TPU v7x, 8 devices: a whole 2x2x1 slice. The times are simulated.
8 devices in a mesh: dp: 1 (over z), tp2: 2 (over y), tp: 4 (over x, core).
Axes of the slice: x: 2, y: 2, z: 1, core: 2. Of those that a mesh axis runs over, the one named last changes fastest.
Arguments:
- hidden: bfloat16 [512, 1536], P('dp')
- w_gate: bfloat16 [1536, 8960], P(None, ('tp', 'tp2'))
- w_up: bfloat16 [1536, 8960], P(None, ('tp', 'tp2'))
- w_down: bfloat16 [8960, 1536], P('tp', 'tp2')
- norm_gain: float32 [1536], replicated
- w_vocab: bfloat16 [1536, 151936], P('tp2', 'tp')
- temperature: float32 [512], P('dp')
- target: int32 [512], P('dp')
Outputs:
- output 1: float32 [512], P('dp')
- output 2: float32 [512], P('dp')
- output 3: float32 [512], P('dp')
- output 4: bfloat16 [512, 151936], P('dp', ('tp', 'tp2'))
All inputs are finite; a program needn't handle non-finite values.
Results may differ from a plain program's by a relative error of at most 0.00875862.
Values are sent between devices in bfloat16 or wider.
A program may use at most 1 GiB of HBM per device.

v0:
```python
import jax
import jax.numpy as jnp
from jax import lax
from jax.sharding import PartitionSpec as P

NORM_EPS = 1e-6


def solution(mesh):
    tp2_size = mesh.shape['tp2']

    def device_step(hidden, w_gate, w_up, w_down, norm_gain, w_vocab, value_a11, target):
        d_model = hidden.shape[1]
        d_local = w_down.shape[1]
        tp_idx = lax.axis_index('tp')
        tp2_idx = lax.axis_index('tp2')
        gate_pre = jnp.dot(hidden, w_gate, preferred_element_type=jnp.float32)
        up_pre = jnp.dot(hidden, w_up, preferred_element_type=jnp.float32)
        act_local = (jax.nn.silu(gate_pre) * up_pre).astype(jnp.bfloat16)
        act_group = lax.all_gather(act_local, 'tp2', axis=1, tiled=True)
        y_part = jnp.dot(act_group, w_down, preferred_element_type=jnp.float32).astype(jnp.bfloat16)
        y_sum = lax.psum(y_part, 'tp')
        hid_local = lax.dynamic_slice_in_dim(hidden, tp2_idx * d_local, d_local, axis=1)
        gain_local = lax.dynamic_slice_in_dim(norm_gain, tp2_idx * d_local, d_local)
        residual = hid_local.astype(jnp.float32) + y_sum.astype(jnp.float32)
        sq_total = lax.psum(jnp.sum(residual * residual, axis=1), 'tp2')
        inv_rms = lax.rsqrt(sq_total / d_model + NORM_EPS)
        normed = (gain_local * residual * inv_rms[:, None]).astype(jnp.bfloat16)
        logit_part = jnp.dot(normed, w_vocab, preferred_element_type=jnp.float32)
        logit_sum = lax.psum_scatter(logit_part, 'tp2', scatter_dimension=1, tiled=True)
        logits = logit_sum / value_a11[:, None]
        v_local = logits.shape[1]
        col_base = (tp_idx * tp2_size + tp2_idx) * v_local
        col_ids = col_base + lax.broadcasted_iota(jnp.int32, (1, v_local), 1)
        local_max = jnp.max(logits, axis=1)
        exp_shift = jnp.exp(logits - local_max[:, None])
        local_sum = jnp.sum(exp_shift, axis=1)
        local_dot = jnp.sum(exp_shift * logits, axis=1)
        local_tgt = jnp.sum(jnp.where(col_ids == target[:, None], logits, 0.0), axis=1)
        glob_max = lax.pmax(local_max, ('tp', 'tp2'))
        rescale = jnp.exp(local_max - glob_max)
        partial_stats = jnp.stack([local_sum * rescale, local_dot * rescale, local_tgt])
        totals = lax.psum(partial_stats, ('tp', 'tp2'))
        log_norm = glob_max + jnp.log(totals[0])
        entropy = log_norm - totals[1] / totals[0]
        tgt_logp = totals[2] - log_norm
        logprobs = (logits - log_norm[:, None]).astype(jnp.bfloat16)
        return log_norm, entropy, tgt_logp, logprobs

    return jax.shard_map(device_step, mesh=mesh, in_specs=(P('dp', None), P(None, ('tp', 'tp2')), P(None, ('tp', 'tp2')), P('tp', 'tp2'), P(None), P('tp2', 'tp'), P('dp'), P('dp')), out_specs=(P('dp'), P('dp'), P('dp'), P('dp', ('tp', 'tp2'))), check_vma=False)
```

profile of v0, /device:TPU:0, one launch (start us, length us, event | category | flops | bytes accessed | tf_op | source)
XLA Modules:
  0.0 1131.7 jit_solution(6845309548036528918)
XLA Ops:
  7.2 0.0 copy-start
  7.2 0.0 all-gather.2.cloned.1.call-start
  7.2 1.9 copy-done
  9.2 3.6 fusion.11
  12.7 0.0 copy-done.2
  12.7 0.0 copy-done.8
  12.7 3.3 fusion.1
  16.0 0.0 all-gather.2.cloned.1.call-update
  16.1 0.0 copy-start.7
  16.1 0.0 copy-start.3
  16.1 0.0 all-reduce.3.cloned.1.call-start
  16.1 35.3 %all-gather.2.cloned.1.call-done = bf16[512,2240]{0,1:T(8,128)(2,1)} async-done(((bf16[512,1120]{0,1:T(8,128)(2,1)}), bf16[512,2240]{0,1:T(8,128)(2,1)}) %all-gather.2.cloned.1.call-update) | async-done | bytes 2293776 | tf_op jit(solution)/shard_map/all_gather | solution.py:20
  51.5 5.6 convolution_convert_fusion
  57.0 0.0 all-reduce.3.cloned.1.call-update
  57.1 0.0 reduce-scatter.4.cloned.1.call-start
  57.1 0.1 dynamic_slice.6
  57.2 29.4 %all-reduce.3.cloned.1.call-done = bf16[512,768]{1,0:T(8,128)(2,1)} async-done(((bf16[512,768]{1,0:T(8,128)(2,1)}), bf16[512,768]{1,0:T(8,128)(2,1)}) %all-reduce.3.cloned.1.call-update) | async-done | bytes 786448 | tf_op jit(solution)/shard_map/psum | solution.py:22
  86.6 0.0 copy-done.3
  86.6 1.5 multiply_reduce_fusion.1
  88.1 5.1 psum.22
  93.2 54.3 %fusion.2 = f32[512,37984]{0,1:T(8,128)} fusion(bf16[768,37984]{0,1:T(8,128)(2,1)} %param.13, bf16[512,768]{1,0:T(8,128)(2,1)} %all-reduce.3.cloned.1.call-done, f32[512]{0:T(512)S(1)} %add_rsqrt_fusion, f32[768]{0:T(1024)S(1)} %dynamic_slice.6, bf16[512,1536]{1,0:T(8,128)(2,1)S(1)} %copy-done.3, s32[]{:T(128)S(6)} %select_n.8), kind=kOutput, calls=%fused_computation.12 | convolution fusion | flops 29874192384 | bytes 137713664 | tf_op jit(solution)/shard_map/dot_general | solution.py:29
  147.4 0.0 reduce-scatter.4.cloned.1.call-update
  147.5 0.0 copy-start.6
  147.5 878.4 %reduce-scatter.4.cloned.1.call-done = f32[512,18992]{0,1:T(8,128)} async-done(((f32[512,37984]{0,1:T(8,128)}), f32[512,18992]{0,1:T(8,128)}) %reduce-scatter.4.cloned.1.call-update) | async-done | bytes 38895632
  1025.9 13.9 %fusion.9 = f32[512]{0:T(512)S(1)} fusion(f32[512,18992]{0,1:T(8,128)} %reduce-scatter.4.cloned.1.call-done, f32[512]{0:T(512)S(1)} %copy-done.4), kind=kLoop, calls=%fused_computation.25 | loop fusion | flops 19447296 | bytes 38899712 | tf_op jit(solution)/shard_map/reduce_max | solution.py:35
  1039.8 22.2 %pmax.7 = f32[512]{0:T(512)S(1)} all-reduce(f32[512]{0:T(512)S(1)} %fusion.9), channel_id=1, replica_groups=mesh['dp'=1,'tp2'=2,'tp'=4] {'tp','tp2'}, use_global_device_ids=true, to_apply=%region_5.6 | all-reduce | flops 512 | bytes 4096 | tf_op jit(solution)/shard_map/pmax | solution.py:40
  1062.1 0.0 copy-done.6
  1062.1 16.8 %fusion = (f32[512]{0:T(512)S(1)}, f32[512]{0:T(512)S(1)}, f32[512]{0:T(512)S(1)}) fusion(f32[512]{0:T(512)S(1)} %fusion.9, f32[512,18992]{0,1:T(8,128)} %reduce-scatter.4.cloned.1.call-done, f32[512]{0:T(512)S(1)} %copy-done.4, s32[512]{0:T(512)S(1)} %copy-done.6, s32[18992]{0:T(1024)S(1)} %iota_add_fusion), kind=kLoop, calls=%fused_computation.4 | loop fusion | flops 77789696 | bytes 38983872 | tf_op jit(solution)/shard_map/reduce_sum | solution.py:37
  1078.9 22.6 %psum.23 = f32[3,512]{1,0:T(4,128)S(1)} all-reduce(f32[3,512]{1,0:T(4,128)S(1)} %pad_maximum_fusion), channel_id=1, replica_groups=mesh['dp'=1,'tp2'=2,'tp'=4] {'tp','tp2'}, use_global_device_ids=true, to_apply=%region_9.10 | all-reduce | flops 1536 | bytes 12288 | tf_op jit(solution)/shard_map/psum | solution.py:43
  1101.5 0.6 fusion.10
  1102.1 0.6 sub.28
  1102.7 22.5 %subtract_convert_fusion = bf16[512,18992]{0,1:T(8,128)(2,1)} fusion(f32[512]{0:T(512)S(1)} %get-tuple-element.8, f32[512,18992]{0,1:T(8,128)} %reduce-scatter.4.cloned.1.call-done, f32[512]{0:T(512)S(1)} %copy-done.4), kind=kLoop, calls=%fused_computation | loop fusion | flops 29171712 | bytes 58347520 | tf_op jit(solution)/shard_map/convert_element_type | solution.py:47
  (14 shorter events, 0.1 us)
Async XLA Ops:
  7.2 2.0 copy-start
  7.2 44.3 %all-gather.2.cloned.1.call-start = ((), (), s32[]{:S(2)}) async-start(), calls=%async_computation.1 | async-start | bytes 3440640 | tf_op jit(solution)/shard_map/all_gather | solution.py:20
  9.1 3.6 copy-start.2
  9.2 3.6 copy-start.8
  16.1 41.1 %copy-start.7 = (f32[1536]{0:T(1024)S(1)}, f32[1536]{0:T(1024)}, u32[]{:S(2)}) copy-start(f32[1536]{0:T(1024)} %param.12) | copy-start | bytes 18436
  16.1 70.5 %copy-start.3 = (bf16[512,1536]{1,0:T(8,128)(2,1)S(1)}, bf16[512,1536]{1,0:T(8,128)(2,1)}, u32[]{:S(2)}) copy-start(bf16[512,1536]{1,0:T(8,128)(2,1)} %param.8) | copy-start | bytes 4718596
  16.1 70.5 %all-reduce.3.cloned.1.call-start = ((), (), s32[]{:S(2)}) async-start(), calls=%async_computation.2 | async-start | bytes 1572864 | tf_op jit(solution)/shard_map/psum | solution.py:22
  57.1 968.8 %reduce-scatter.4.cloned.1.call-start = ((), (), s32[]{:S(2)}) async-start(), calls=%async_computation.3 | async-start | bytes 116686848
  147.4 878.5 %copy-start.4 = (f32[512]{0:T(512)S(1)}, f32[512]{0:T(512)}, u32[]{:S(2)}) copy-start(f32[512]{0:T(512)} %param.14) | copy-start | bytes 6148
  147.5 914.6 %copy-start.6 = (s32[512]{0:T(512)S(1)}, s32[512]{0:T(512)}, u32[]{:S(2)}) copy-start(s32[512]{0:T(512)} %param.15) | copy-start | bytes 6148
  1102.1 23.1 %copy-start.5 = (f32[512]{0:T(512)}, f32[512]{0:T(512)S(1)}, u32[]{:S(2)}) copy-start(f32[512]{0:T(512)S(1)} %get-tuple-element.8) | copy-start | bytes 6148
  1102.7 22.5 %copy-start.1 = (bf16[1536,1120]{0,1:T(8,128)(2,1)S(1)}, bf16[1536,1120]{0,1:T(8,128)(2,1)}, u32[]{:S(2)}) copy-start(bf16[1536,1120]{0,1:T(8,128)(2,1)} %param.9) | copy-start | bytes 10321924
Sparse Core Ops, SparseCore 0:
  16.2 35.2 all-gather.1
  57.2 29.3 all-reduce.2
  147.6 878.2 reduce-scatter.3
where the time goes:
time: 1130 us
  waiting for transfers between devices  943 us (83%)
  matrix products  66.7 us (6%)
  other arithmetic  55.9 us (5%)
  blocking collectives  49.9 us (4%)
  between operations  13.9 us (1%)
    unnamed x4, waiting for transfers between devices  878 us
    dot_general x1, matrix products, device_step(): logit_part = jnp.dot(normed, w_vocab, preferred_element_type=jnp.float32)  54.3 us
    all_gather x1, waiting for transfers between devices, device_step(): act_group = lax.all_gather(act_local, 'tp2', axis=1, tiled=True)  35.3 us
    psum x1, waiting for transfers between devices, device_step(): y_sum = lax.psum(y_part, 'tp')  29.4 us
  transfers between devices with their start and end apart: 3, of which 3 were waited for; matrix products, arithmetic and copies ran while one was open for 0% of the time, Pallas kernels for 0%

commit v1 on v0

v1 whole, which is shorter than its diff:
```python
import functools

import jax
import jax.numpy as jnp
from jax import lax
from jax.experimental import pallas as pl
from jax.experimental.pallas import tpu as pltpu
from jax.sharding import PartitionSpec as P

NORM_EPS = 1e-6
NEG = float(jnp.finfo(jnp.float32).min)
MESH = pl.DeviceIdType.MESH
CHUNK = 512
SUB = 64
EARLY = 8
DEPTH = 3
BLOCK = 1024


def nt(a, b):
    return lax.dot_general(a, b, (((1,), (1,)), ((), ())), preferred_element_type=jnp.float32)


def tn(a, b):
    return lax.dot_general(a, b, (((0,), (0,)), ((), ())), preferred_element_type=jnp.float32)


def nn(a, b):
    return jnp.dot(a, b, preferred_element_type=jnp.float32)


def head_kernel(n_tp, v_l,
                hidden, wg, wu, wd, gain, temp, target, wv,
                logits, recv,
                hid_v, wg_v, wu_v, wd_v, temp_v, tgt_v, gain_v,
                a_own, a_oth, y_part, y_recv, y_sum, y_oth, x_v, x_t, w_own, w_oth,
                run_m, run_s, run_d, run_t, st_all,
                load_sem, w_send, w_got, a_sem, y_send, y_got, s_sem, x_send, x_got,
                own_sem, oth_sem, st_send, st_got):
    _, rb, d_model = hid_v.shape
    ff_l = wg_v.shape[0]
    d_l = d_model // 2
    rows = n_tp * rb
    n_full = v_l // CHUNK
    rest = v_l - n_full * CHUNK
    tp = lax.axis_index('tp')
    y = lax.axis_index('tp2')
    oy = 1 - y
    me = tp * 2 + y
    other = {'tp2': oy}
    peers = [(dt, dy) for dt in range(n_tp) for dy in range(2) if dt or dy]

    def dev(dt, dy):
        return {'tp': lax.rem(tp + dt, n_tp), 'tp2': lax.rem(y + dy, 2)}

    barrier = pltpu.get_barrier_semaphore()
    for dt, dy in peers:
        pl.semaphore_signal(barrier, inc=1, device_id=dev(dt, dy), device_id_type=MESH)
    pl.semaphore_wait(barrier, len(peers))

    def ship(c, width=CHUNK):
        row = c * CHUNK
        return pltpu.make_async_remote_copy(
            src_ref=wv.at[pl.ds(pl.multiple_of(oy * v_l + row, 16), width), :],
            dst_ref=recv.at[pl.ds(pl.multiple_of(row, 16), width), :],
            send_sem=w_send.at[c], recv_sem=w_got.at[c],
            device_id=other, device_id_type=MESH)

    ship(0).start()

    def load(src, dst, k):
        cp = pltpu.make_async_copy(src, dst, load_sem.at[k])
        cp.start()
        return cp

    own_ff = pl.ds(pl.multiple_of(y * ff_l, 16), ff_l)
    oth_ff = pl.ds(pl.multiple_of(oy * ff_l, 16), ff_l)
    loads = [load(hidden, hid_v, 0), load(wg, wg_v, 1), load(wu, wu_v, 2),
             load(wd.at[own_ff, :], wd_v.at[0], 3), load(wd.at[oth_ff, :], wd_v.at[1], 4),
             load(temp, temp_v, 5), load(target, tgt_v, 6), load(gain, gain_v, 7)]
    for cp in loads:
        cp.wait()

    part = ff_l // 5

    @pl.loop(0, 5)
    def _(j):
        fs = pl.ds(pl.multiple_of(j * part, 16), part)
        h = hid_v[...].reshape(rows, d_model)
        g = nt(wg_v[fs, :], h)
        u = nt(wu_v[fs, :], h)
        a_own[fs, :] = (g * (1.0 / (1.0 + jnp.exp(-g))) * u).astype(jnp.bfloat16)

    a_copy = pltpu.make_async_remote_copy(
        src_ref=a_own, dst_ref=a_oth, send_sem=a_sem.at[0], recv_sem=a_sem.at[1],
        device_id=other, device_id_type=MESH)
    a_copy.start()
    for c in range(1, 4):
        ship(c).start()

    run_m[...] = jnp.full(run_m.shape, NEG, jnp.float32)
    run_s[...] = jnp.zeros(run_s.shape, jnp.float32)
    run_d[...] = jnp.zeros(run_d.shape, jnp.float32)
    run_t[...] = jnp.zeros(run_t.shape, jnp.float32)
    a_copy.wait()

    for q in range(n_tp):
        qs = slice(q * rb, (q + 1) * rb)
        acc = tn(a_own[:, qs], wd_v[0]) + tn(a_oth[:, qs], wd_v[1])
        y_part[q] = acc.astype(jnp.bfloat16)

    y_copies = []
    for o in range(1, n_tp):
        to = lax.rem(tp + o, n_tp)
        cp = pltpu.make_async_remote_copy(
            src_ref=y_part.at[to], dst_ref=y_recv.at[o - 1],
            send_sem=y_send.at[o - 1], recv_sem=y_got.at[o - 1],
            device_id={'tp': to}, device_id_type=MESH)
        cp.start()
        y_copies.append(cp)
    for cp in y_copies:
        cp.wait()
    total = y_part[tp].astype(jnp.float32)
    for o in range(n_tp - 1):
        total += y_recv[o].astype(jnp.float32)
    y_sum[...] = total.astype(jnp.bfloat16)
    s_copy = pltpu.make_async_remote_copy(
        src_ref=y_sum, dst_ref=y_oth, send_sem=s_sem.at[0], recv_sem=s_sem.at[1],
        device_id=other, device_id_type=MESH)
    s_copy.start()
    for c in range(4, EARLY):
        ship(c).start()
    s_copy.wait()

    mine = y_sum[...].astype(jnp.float32)
    theirs = y_oth[...].astype(jnp.float32)
    first = jnp.zeros(mine.shape, jnp.int32) + y == 0
    h = hid_v[tp].astype(jnp.float32)
    r0 = h[:, :d_l] + jnp.where(first, mine, theirs)
    r1 = h[:, d_l:] + jnp.where(first, theirs, mine)
    sq = jnp.sum(r0 * r0, axis=1, keepdims=True) + jnp.sum(r1 * r1, axis=1, keepdims=True)
    inv = lax.rsqrt(sq / d_model + NORM_EPS)
    x_v[tp, :, :d_l] = (gain_v[:, :d_l] * r0 * inv).astype(jnp.bfloat16)
    x_v[tp, :, d_l:] = (gain_v[:, d_l:] * r1 * inv).astype(jnp.bfloat16)
    x_copies = []
    for o in range(1, n_tp):
        to = lax.rem(tp + o, n_tp)
        cp = pltpu.make_async_remote_copy(
            src_ref=x_v.at[tp], dst_ref=x_v.at[tp],
            send_sem=x_send.at[o - 1], recv_sem=x_got.at[o - 1],
            device_id={'tp': to}, device_id_type=MESH)
        cp.start()
        x_copies.append(cp)
    for cp in x_copies:
        cp.wait()
    for q in range(n_tp):
        qs = slice(q * rb, (q + 1) * rb)
        for s in range(2):
            block = x_v[q, :, s * d_l:(s + 1) * d_l].astype(jnp.float32)
            x_t[s, :, qs] = block.T.astype(jnp.bfloat16)

    def own(c, slot, width=CHUNK):
        return pltpu.make_async_copy(
            wv.at[pl.ds(pl.multiple_of(y * v_l + c * CHUNK, 16), width), :],
            w_own.at[slot, pl.ds(0, width), :], own_sem.at[slot])

    def came(c, slot, width=CHUNK):
        return pltpu.make_async_copy(
            recv.at[pl.ds(pl.multiple_of(c * CHUNK, 16), width), :],
            w_oth.at[slot, pl.ds(0, width), :], oth_sem)

    inv_t = 1.0 / temp_v[...]
    local_t = tgt_v[...] - me * v_l

    def update(base, width):
        lg = logits[pl.ds(pl.multiple_of(base, 16), width), :]
        tiles = lg.reshape(width // 8, 8, rows)
        ids = lax.broadcasted_iota(jnp.int32, (width, rows), 0)
        hit = jnp.where(ids == local_t - base, lg, 0.0).reshape(width // 8, 8, rows)
        m_old = run_m[...]
        m_new = jnp.maximum(m_old, jnp.max(tiles, axis=0))
        keep = jnp.exp(m_old - m_new)
        p = jnp.exp(tiles - m_new[None])
        run_m[...] = m_new
        run_s[...] = run_s[...] * keep + jnp.sum(p, axis=0)
        run_d[...] = run_d[...] * keep + jnp.sum(p * tiles, axis=0)
        run_t[...] += jnp.sum(hit, axis=0)

    def multiply(c, slot, width=CHUNK):
        ws = pl.ds(0, width)
        acc = nn(w_own[slot, ws, :], x_t[y]) + nn(w_oth[slot, ws, :], x_t[oy])
        logits[pl.ds(pl.multiple_of(c * CHUNK, 16), width), :] = acc * inv_t

    own(0, 0).start()

    @pl.loop(0, n_full)
    def _(c):
        slot = lax.rem(c, 2)
        after = lax.rem(c + 1, 2)

        @pl.when(c + 1 < n_full)
        def _():
            own(c + 1, after).start()

        @pl.when(c + 1 == n_full)
        def _():
            own(n_full, n_full % 2, rest).start()

        @pl.when((c + DEPTH >= EARLY) & (c + DEPTH < n_full))
        def _():
            ship(c + DEPTH).start()

        @pl.when(c + DEPTH == n_full)
        def _():
            ship(n_full, rest).start()

        own(c, slot).wait()
        ship(c).wait()
        copy = came(c, slot)
        copy.start()
        copy.wait()
        multiply(c, slot)

        @pl.loop(0, CHUNK // SUB)
        def _(k):
            update(c * CHUNK + k * SUB, SUB)

    slot = n_full % 2
    own(n_full, slot, rest).wait()
    ship(n_full, rest).wait()
    copy = came(n_full, slot, rest)
    copy.start()
    copy.wait()
    multiply(n_full, slot, rest)
    update(n_full * CHUNK, rest)

    m = run_m[...]
    top = jnp.max(m, axis=0, keepdims=True)
    keep = jnp.exp(m - top)
    st_all[me, 0:1, :] = top
    st_all[me, 1:2, :] = jnp.sum(run_s[...] * keep, axis=0, keepdims=True)
    st_all[me, 2:3, :] = jnp.sum(run_d[...] * keep, axis=0, keepdims=True)
    st_all[me, 3:4, :] = jnp.sum(run_t[...], axis=0, keepdims=True)
    st_all[me, 4:8, :] = jnp.zeros((4, rows), jnp.float32)
    st_copies = []
    for i, (dt, dy) in enumerate(peers):
        cp = pltpu.make_async_remote_copy(
            src_ref=st_all.at[me], dst_ref=st_all.at[me],
            send_sem=st_send.at[i], recv_sem=st_got.at[i],
            device_id=dev(dt, dy), device_id_type=MESH)
        cp.start()
        st_copies.append(cp)
    for cp in st_copies:
        cp.wait()
    n_dev = n_tp * 2
    g_max = st_all[0, 0:1, :]
    for i in range(1, n_dev):
        g_max = jnp.maximum(g_max, st_all[i, 0:1, :])
    tot_s = jnp.zeros_like(g_max)
    tot_d = jnp.zeros_like(g_max)
    tot_t = jnp.zeros_like(g_max)
    for i in range(n_dev):
        w = jnp.exp(st_all[i, 0:1, :] - g_max)
        tot_s += w * st_all[i, 1:2, :]
        tot_d += w * st_all[i, 2:3, :]
        tot_t += st_all[i, 3:4, :]
    log_norm = g_max + jnp.log(tot_s)
    logits[v_l:v_l + 1, :] = log_norm
    logits[v_l + 1:v_l + 2, :] = log_norm - tot_d / tot_s
    logits[v_l + 2:v_l + 3, :] = tot_t - log_norm
    logits[v_l + 3:v_l + 8, :] = jnp.zeros((5, rows), jnp.float32)


def out_kernel(v_l, logits, out, stats):
    i = pl.program_id(0)
    n_full = v_l // BLOCK
    rest = v_l - n_full * BLOCK

    def put(at, width):
        lg = logits[pl.ds(pl.multiple_of(i * BLOCK + at, 16), width), :]
        out[pl.ds(pl.multiple_of(at, 16), width), :] = (lg - logits[v_l:v_l + 1, :]).astype(jnp.bfloat16)

    @pl.when(i == 0)
    def _():
        stats[...] = logits[v_l:v_l + 8, :]

    @pl.when(i < n_full)
    def _():
        @pl.loop(0, BLOCK // 128)
        def _(k):
            put(k * 128, 128)

    @pl.when(i == n_full)
    def _():
        @pl.loop(0, rest // 112)
        def _(k):
            put(k * 112, 112)


def solution(mesh):
    n_tp = mesh.shape['tp']

    def device_step(hidden, w_gate, w_up, w_down, norm_gain, w_vocab, temperature, target):
        rows, d_model = hidden.shape
        ff_l = w_gate.shape[1]
        d_l = w_down.shape[1]
        v_l = w_vocab.shape[1] // 2
        rb = rows // n_tp
        n_sends = v_l // CHUNK + 1
        any_spec = pl.BlockSpec(memory_space=pl.ANY)
        vmem_spec = pl.BlockSpec(memory_space=pltpu.VMEM)
        bf, f32 = jnp.bfloat16, jnp.float32
        dma = pltpu.SemaphoreType.DMA
        logits, _ = pl.pallas_call(
            functools.partial(head_kernel, n_tp, v_l),
            out_shape=(pltpu.VMEM((v_l + 8, rows), f32),
                       jax.ShapeDtypeStruct((v_l, d_l), bf)),
            in_specs=[any_spec] * 8,
            out_specs=(vmem_spec, any_spec),
            scratch_shapes=[
                pltpu.VMEM((n_tp, rb, d_model), bf),
                pltpu.VMEM((ff_l, d_model), bf),
                pltpu.VMEM((ff_l, d_model), bf),
                pltpu.VMEM((2, ff_l, d_l), bf),
                pltpu.VMEM((1, rows), f32),
                pltpu.VMEM((1, rows), jnp.int32),
                pltpu.VMEM((1, d_model), f32),
                pltpu.VMEM((ff_l, rows), bf),
                pltpu.VMEM((ff_l, rows), bf),
                pltpu.VMEM((n_tp, rb, d_l), bf),
                pltpu.VMEM((n_tp - 1, rb, d_l), bf),
                pltpu.VMEM((rb, d_l), bf),
                pltpu.VMEM((rb, d_l), bf),
                pltpu.VMEM((n_tp, rb, d_model), bf),
                pltpu.VMEM((2, d_l, rows), bf),
                pltpu.VMEM((2, CHUNK, d_l), bf),
                pltpu.VMEM((2, CHUNK, d_l), bf),
                pltpu.VMEM((8, rows), f32),
                pltpu.VMEM((8, rows), f32),
                pltpu.VMEM((8, rows), f32),
                pltpu.VMEM((8, rows), f32),
                pltpu.VMEM((n_tp * 2, 8, rows), f32),
                dma((8,)), dma((n_sends,)), dma((n_sends,)), dma((2,)),
                dma((n_tp - 1,)), dma((n_tp - 1,)), dma((2,)),
                dma((n_tp - 1,)), dma((n_tp - 1,)),
                dma((2,)), dma(()), dma((7,)), dma((7,)),
            ],
            compiler_params=pltpu.CompilerParams(
                collective_id=0, has_side_effects=True, vmem_limit_bytes=25 * 2 ** 20),
        )(hidden.reshape(n_tp, rb, d_model), w_gate.T, w_up.T, w_down, norm_gain.reshape(1, -1),
          temperature.reshape(1, -1), target.reshape(1, -1), w_vocab.T)
        logprobs, stats = pl.pallas_call(
            functools.partial(out_kernel, v_l),
            grid=(pl.cdiv(v_l, BLOCK),),
            out_shape=(pltpu.HBM((v_l, rows), bf), pltpu.HBM((8, rows), f32)),
            in_specs=[vmem_spec],
            out_specs=(pl.BlockSpec((BLOCK, rows), lambda i: (i, 0)), vmem_spec),
            compiler_params=pltpu.CompilerParams(vmem_limit_bytes=8 * 2 ** 20),
        )(logits)
        return stats[0], stats[1], stats[2], logprobs.T

    return jax.shard_map(device_step, mesh=mesh, in_specs=(P('dp', None), P(None, ('tp', 'tp2')), P(None, ('tp', 'tp2')), P('tp', 'tp2'), P(None), P('tp2', 'tp'), P('dp'), P('dp')), out_specs=(P('dp'), P('dp'), P('dp'), P('dp', ('tp', 'tp2'))), check_vma=False)
```

time: 1130 us -> 683 us (0.60)
  waiting for transfers between devices: 943 us -> 0 us
  Pallas kernels: 0 us -> 678 us
  matrix products: 66.7 us -> 0 us
  other arithmetic: 55.9 us -> 0 us
  blocking collectives: 49.9 us -> 0 us
  between operations: 13.9 us -> 0.64 us
    unnamed x4 -> x0, waiting for transfers between devices: 878 us -> none
    pallas_call x0 -> x2, Pallas kernels: none -> 678 us  [the longest x1 667 us: device_step(): pl.pallas_call(functools.partial(head_kernel, n_tp, v_l), out_shape=(pltp...]
    dot_general x4 -> x0, matrix products: 66.7 us -> none  [the longest x1 54.3 us: device_step(): logit_part = jnp.dot(normed, w_vocab, preferred_element_type=jnp.float32)]
    all_gather x1 -> x0, waiting for transfers between devices: 35.3 us -> none  [device_step(): act_group = lax.all_gather(act_local, 'tp2', axis=1, tiled=True)]
    psum x1 -> x0, waiting for transfers between devices: 29.4 us -> none  [device_step(): y_sum = lax.psum(y_part, 'tp')]
    psum x2 -> x0, blocking collectives: 27.7 us -> none  [the longest x1 22.6 us: device_step(): totals = lax.psum(partial_stats, ('tp', 'tp2'))]
    convert_element_type x1 -> x0, other arithmetic: 22.5 us -> none  [device_step(): logprobs = (logits - log_norm[:, None]).astype(jnp.bfloat16)]
    pmax x1 -> x0, blocking collectives: 22.2 us -> none  [device_step(): glob_max = lax.pmax(local_max, ('tp', 'tp2'))]
  transfers between devices with their start and end apart: 3 -> 0, of which waited for: 3 -> 0; matrix products, arithmetic and copies ran while one was open for 0% -> 0% of each run, Pallas kernels for 0% -> 0%
where the time goes in v1:
time: 683 us; the launch traced here: 682 us
  Pallas kernels  678 us (99%)
    pallas_call x1, Pallas kernels, device_step(): pl.pallas_call(functools.partial(head_kernel, n_tp, v_l), out_shape=(pltp...  667 us

profile of v1, /device:TPU:0, one launch (start us, length us, event | category | flops | bytes accessed | tf_op | source)
XLA Modules:
  0.0 681.6 jit_solution(6603900558426763774)
XLA Ops:
  0.6 1.3 reshape.21.gain
  1.9 667.1 %shard_map.111 = (f32[19000,512]{1,0:T(8,128)S(1)}, bf16[18992,768]{1,0:T(8,128)(2,1)}) custom-call(bf16[4,128,1536]{2,1,0:T(8,128)(2,1)} %bitcast.13, bf16[1120,1536]{1,0:T(8,128)(2,1)} %bitcast.11, bf16[1120,1536]{1,0:T(8,128)(2,1)} %bitcast.12, bf16[2240,768]{1,0:T(8,128)(2,1)} %wd.1, f32[1,1536]{1,0:T(1,128)} %reshape.21.gain, f32[1,512]{1,0:T(1,128)} %bitcast.14, ...), custom_call_target="tpu_custom_call" | custom-call | tf_op jit(solution)/shard_map/pallas_call | solution.py:314
  669.1 11.1 %shard_map.112 = (bf16[18992,512]{1,0:T(8,128)(2,1)}, f32[8,512]{1,0:T(8,128)}) custom-call(f32[19000,512]{1,0:T(8,128)S(1)} %get-tuple-element.7.logits), custom_call_target="tpu_custom_call" | custom-call | tf_op jit(solution)/shard_map/pallas_call | solution.py:352
  680.1 1.4 fusion

commit v2 on v1

--- a/solution.py
+++ b/solution.py
@@ -12,9 +12,10 @@
 MESH = pl.DeviceIdType.MESH
 CHUNK = 512
 SUB = 64
-EARLY = 8
+EARLY = 10
 DEPTH = 3
-BLOCK = 1024
+BLOCK = 512
+SLOTS = 6
 
 
 def nt(a, b):
@@ -29,20 +30,20 @@
     return jnp.dot(a, b, preferred_element_type=jnp.float32)
 
 
-def head_kernel(n_tp, v_l,
+def head_kernel(n_tp, v_l, ends,
                 hidden, wg, wu, wd, gain, temp, target, wv,
                 logits, recv,
                 hid_v, wg_v, wu_v, wd_v, temp_v, tgt_v, gain_v,
-                a_own, a_oth, y_part, y_recv, y_sum, y_oth, x_v, x_t, w_own, w_oth,
+                a_own, a_oth, y_part, y_recv, y_sum, y_oth, x_v, x_t, w_own, w_oth, e_own, e_oth,
                 run_m, run_s, run_d, run_t, st_all,
                 load_sem, w_send, w_got, a_sem, y_send, y_got, s_sem, x_send, x_got,
-                own_sem, oth_sem, st_send, st_got):
+                own_sem, oth_sem, end_sem, st_send, st_got):
     _, rb, d_model = hid_v.shape
     ff_l = wg_v.shape[0]
     d_l = d_model // 2
     rows = n_tp * rb
-    n_full = v_l // CHUNK
-    rest = v_l - n_full * CHUNK
+    n_end = sum(ends)
+    n_full = (v_l - n_end) // CHUNK
     tp = lax.axis_index('tp')
     y = lax.axis_index('tp2')
     oy = 1 - y
@@ -58,15 +59,22 @@
         pl.semaphore_signal(barrier, inc=1, device_id=dev(dt, dy), device_id_type=MESH)
     pl.semaphore_wait(barrier, len(peers))
 
-    def ship(c, width=CHUNK):
-        row = c * CHUNK
+    def send(row, width, dst, k):
         return pltpu.make_async_remote_copy(
             src_ref=wv.at[pl.ds(pl.multiple_of(oy * v_l + row, 16), width), :],
-            dst_ref=recv.at[pl.ds(pl.multiple_of(row, 16), width), :],
-            send_sem=w_send.at[c], recv_sem=w_got.at[c],
+            dst_ref=dst, send_sem=w_send.at[k], recv_sem=w_got.at[k],
             device_id=other, device_id_type=MESH)
 
+    def ship(c):
+        row = c * CHUNK
+        return send(row, CHUNK, recv.at[pl.ds(pl.multiple_of(row, 16), CHUNK), :], c)
+
+    def ship_end(i):
+        at = sum(ends[:i])
+        return send(n_full * CHUNK + at, ends[i], e_oth.at[pl.ds(at, ends[i]), :], n_full + i)
+
     ship(0).start()
+    ship(1).start()
 
     def load(src, dst, k):
         cp = pltpu.make_async_copy(src, dst, load_sem.at[k])
@@ -95,7 +103,7 @@
         src_ref=a_own, dst_ref=a_oth, send_sem=a_sem.at[0], recv_sem=a_sem.at[1],
         device_id=other, device_id_type=MESH)
     a_copy.start()
-    for c in range(1, 4):
+    for c in range(2, 6):
         ship(c).start()
 
     run_m[...] = jnp.full(run_m.shape, NEG, jnp.float32)
@@ -128,7 +136,7 @@
         src_ref=y_sum, dst_ref=y_oth, send_sem=s_sem.at[0], recv_sem=s_sem.at[1],
         device_id=other, device_id_type=MESH)
     s_copy.start()
-    for c in range(4, EARLY):
+    for c in range(6, EARLY):
         ship(c).start()
     s_copy.wait()
 
@@ -140,8 +148,10 @@
     r1 = h[:, d_l:] + jnp.where(first, theirs, mine)
     sq = jnp.sum(r0 * r0, axis=1, keepdims=True) + jnp.sum(r1 * r1, axis=1, keepdims=True)
     inv = lax.rsqrt(sq / d_model + NORM_EPS)
-    x_v[tp, :, :d_l] = (gain_v[:, :d_l] * r0 * inv).astype(jnp.bfloat16)
-    x_v[tp, :, d_l:] = (gain_v[:, d_l:] * r1 * inv).astype(jnp.bfloat16)
+    for k in range(d_model // 128):
+        half, at = (r0, k * 128) if k * 128 < d_l else (r1, k * 128 - d_l)
+        block = gain_v[k:k + 1, :] * half[:, at:at + 128] * inv
+        x_v[tp, :, k * 128:(k + 1) * 128] = block.astype(jnp.bfloat16)
     x_copies = []
     for o in range(1, n_tp):
         to = lax.rem(tp + o, n_tp)
@@ -159,15 +169,13 @@
             block = x_v[q, :, s * d_l:(s + 1) * d_l].astype(jnp.float32)
             x_t[s, :, qs] = block.T.astype(jnp.bfloat16)
 
-    def own(c, slot, width=CHUNK):
+    def own(c, slot):
         return pltpu.make_async_copy(
-            wv.at[pl.ds(pl.multiple_of(y * v_l + c * CHUNK, 16), width), :],
-            w_own.at[slot, pl.ds(0, width), :], own_sem.at[slot])
-
-    def came(c, slot, width=CHUNK):
-        return pltpu.make_async_copy(
-            recv.at[pl.ds(pl.multiple_of(c * CHUNK, 16), width), :],
-            w_oth.at[slot, pl.ds(0, width), :], oth_sem)
+            wv.at[pl.ds(pl.multiple_of(y * v_l + c * CHUNK, 16), CHUNK), :],
+            w_own.at[slot], own_sem.at[slot])
+
+    own_end = pltpu.make_async_copy(
+        wv.at[pl.ds(pl.multiple_of(y * v_l + n_full * CHUNK, 16), n_end), :], e_own, end_sem)
 
     inv_t = 1.0 / temp_v[...]
     local_t = tgt_v[...] - me * v_l
@@ -186,53 +194,50 @@
         run_d[...] = run_d[...] * keep + jnp.sum(p * tiles, axis=0)
         run_t[...] += jnp.sum(hit, axis=0)
 
-    def multiply(c, slot, width=CHUNK):
-        ws = pl.ds(0, width)
-        acc = nn(w_own[slot, ws, :], x_t[y]) + nn(w_oth[slot, ws, :], x_t[oy])
-        logits[pl.ds(pl.multiple_of(c * CHUNK, 16), width), :] = acc * inv_t
-
+    own_end.start()
     own(0, 0).start()
 
     @pl.loop(0, n_full)
     def _(c):
         slot = lax.rem(c, 2)
-        after = lax.rem(c + 1, 2)
 
         @pl.when(c + 1 < n_full)
         def _():
-            own(c + 1, after).start()
-
-        @pl.when(c + 1 == n_full)
-        def _():
-            own(n_full, n_full % 2, rest).start()
+            own(c + 1, lax.rem(c + 1, 2)).start()
 
         @pl.when((c + DEPTH >= EARLY) & (c + DEPTH < n_full))
         def _():
             ship(c + DEPTH).start()
 
-        @pl.when(c + DEPTH == n_full)
-        def _():
-            ship(n_full, rest).start()
+        for i in range(len(ends)):
+            @pl.when(c + DEPTH == n_full + i)
+            def _():
+                ship_end(i).start()
 
         own(c, slot).wait()
         ship(c).wait()
-        copy = came(c, slot)
-        copy.start()
-        copy.wait()
-        multiply(c, slot)
+        came = pltpu.make_async_copy(
+            recv.at[pl.ds(pl.multiple_of(c * CHUNK, 16), CHUNK), :], w_oth.at[slot], oth_sem)
+        came.start()
+        came.wait()
+        acc = nn(w_own[slot], x_t[y]) + nn(w_oth[slot], x_t[oy])
+        logits[pl.ds(pl.multiple_of(c * CHUNK, 16), CHUNK), :] = acc * inv_t
 
         @pl.loop(0, CHUNK // SUB)
         def _(k):
             update(c * CHUNK + k * SUB, SUB)
 
-    slot = n_full % 2
-    own(n_full, slot, rest).wait()
-    ship(n_full, rest).wait()
-    copy = came(n_full, slot, rest)
-    copy.start()
-    copy.wait()
-    multiply(n_full, slot, rest)
-    update(n_full * CHUNK, rest)
+    at = n_full * CHUNK
+    own_end.wait()
+    logits[at:at + n_end, :] = nn(e_own[...], x_t[y])
+    for i, n in enumerate(ends):
+        ship_end(i).wait()
+        es = slice(at - n_full * CHUNK, at - n_full * CHUNK + n)
+        logits[at:at + n, :] = (logits[at:at + n, :] + nn(e_oth[es, :], x_t[oy])) * inv_t
+        steps = -(-n // 128)
+        for k in range(steps):
+            update(at + k * (n // steps), n // steps)
+        at += n
 
     m = run_m[...]
     top = jnp.max(m, axis=0, keepdims=True)
@@ -271,30 +276,45 @@
     logits[v_l + 3:v_l + 8, :] = jnp.zeros((5, rows), jnp.float32)
 
 
-def out_kernel(v_l, logits, out, stats):
-    i = pl.program_id(0)
+def out_kernel(v_l, logits, out, log_norm, entropy, target_lp, buf, row0, row1, row2, sem, row_sem):
     n_full = v_l // BLOCK
     rest = v_l - n_full * BLOCK
-
-    def put(at, width):
-        lg = logits[pl.ds(pl.multiple_of(i * BLOCK + at, 16), width), :]
-        out[pl.ds(pl.multiple_of(at, 16), width), :] = (lg - logits[v_l:v_l + 1, :]).astype(jnp.bfloat16)
-
-    @pl.when(i == 0)
-    def _():
-        stats[...] = logits[v_l:v_l + 8, :]
-
-    @pl.when(i < n_full)
-    def _():
-        @pl.loop(0, BLOCK // 128)
-        def _(k):
-            put(k * 128, 128)
-
-    @pl.when(i == n_full)
-    def _():
-        @pl.loop(0, rest // 112)
-        def _(k):
-            put(k * 112, 112)
+    row_copies = []
+    for k, (row, dst) in enumerate(((row0, log_norm), (row1, entropy), (row2, target_lp))):
+        row[...] = logits[v_l + k:v_l + k + 1, :]
+        cp = pltpu.make_async_copy(row, dst, row_sem.at[k])
+        cp.start()
+        row_copies.append(cp)
+
+    def put(b, slot, width=BLOCK):
+        return pltpu.make_async_copy(
+            buf.at[slot, pl.ds(0, width), :],
+            out.at[pl.ds(pl.multiple_of(b * BLOCK, 16), width), :], sem.at[slot])
+
+    def fill(b, slot, width=BLOCK):
+        lg = logits[pl.ds(pl.multiple_of(b * BLOCK, 16), width), :]
+        buf[slot, :width, :] = (lg - row0[...]).astype(jnp.bfloat16)
+
+    @pl.loop(0, n_full)
+    def _(b):
+        slot = lax.rem(b, SLOTS)
+
+        @pl.when(b >= SLOTS)
+        def _():
+            put(b - SLOTS, slot).wait()
+
+        fill(b, slot)
+        put(b, slot).start()
+
+    slot = n_full % SLOTS
+    put(n_full - SLOTS, slot).wait()
+    fill(n_full, slot, rest)
+    put(n_full, slot, rest).start()
+    for b in range(n_full - SLOTS + 1, n_full):
+        put(b, b % SLOTS).wait()
+    put(n_full, slot, rest).wait()
+    for cp in row_copies:
+        cp.wait()
 
 
 def solution(mesh):
@@ -306,13 +326,15 @@
         d_l = w_down.shape[1]
         v_l = w_vocab.shape[1] // 2
         rb = rows // n_tp
-        n_sends = v_l // CHUNK + 1
+        over = v_l % CHUNK + CHUNK
+        ends = (over - 224, 160, 64)
+        n_sends = v_l // CHUNK - 1 + len(ends)
         any_spec = pl.BlockSpec(memory_space=pl.ANY)
         vmem_spec = pl.BlockSpec(memory_space=pltpu.VMEM)
         bf, f32 = jnp.bfloat16, jnp.float32
         dma = pltpu.SemaphoreType.DMA
         logits, _ = pl.pallas_call(
-            functools.partial(head_kernel, n_tp, v_l),
+            functools.partial(head_kernel, n_tp, v_l, ends),
             out_shape=(pltpu.VMEM((v_l + 8, rows), f32),
                        jax.ShapeDtypeStruct((v_l, d_l), bf)),
             in_specs=[any_spec] * 8,
@@ -324,7 +346,7 @@
                 pltpu.VMEM((2, ff_l, d_l), bf),
                 pltpu.VMEM((1, rows), f32),
                 pltpu.VMEM((1, rows), jnp.int32),
-                pltpu.VMEM((1, d_model), f32),
+                pltpu.VMEM((d_model // 128, 128), f32),
                 pltpu.VMEM((ff_l, rows), bf),
                 pltpu.VMEM((ff_l, rows), bf),
                 pltpu.VMEM((n_tp, rb, d_l), bf),
@@ -335,6 +357,8 @@
                 pltpu.VMEM((2, d_l, rows), bf),
                 pltpu.VMEM((2, CHUNK, d_l), bf),
                 pltpu.VMEM((2, CHUNK, d_l), bf),
+                pltpu.VMEM((over, d_l), bf),
+                pltpu.VMEM((over, d_l), bf),
                 pltpu.VMEM((8, rows), f32),
                 pltpu.VMEM((8, rows), f32),
                 pltpu.VMEM((8, rows), f32),
@@ -343,20 +367,22 @@
                 dma((8,)), dma((n_sends,)), dma((n_sends,)), dma((2,)),
                 dma((n_tp - 1,)), dma((n_tp - 1,)), dma((2,)),
                 dma((n_tp - 1,)), dma((n_tp - 1,)),
-                dma((2,)), dma(()), dma((7,)), dma((7,)),
+                dma((2,)), dma(()), dma(()), dma((7,)), dma((7,)),
             ],
             compiler_params=pltpu.CompilerParams(
                 collective_id=0, has_side_effects=True, vmem_limit_bytes=25 * 2 ** 20),
-        )(hidden.reshape(n_tp, rb, d_model), w_gate.T, w_up.T, w_down, norm_gain.reshape(1, -1),
+        )(hidden.reshape(n_tp, rb, d_model), w_gate.T, w_up.T, w_down, norm_gain.reshape(-1, 128),
           temperature.reshape(1, -1), target.reshape(1, -1), w_vocab.T)
-        logprobs, stats = pl.pallas_call(
+        row = pltpu.HBM((1, rows), f32)
+        logprobs, log_norm, entropy, target_lp = pl.pallas_call(
             functools.partial(out_kernel, v_l),
-            grid=(pl.cdiv(v_l, BLOCK),),
-            out_shape=(pltpu.HBM((v_l, rows), bf), pltpu.HBM((8, rows), f32)),
+            out_shape=(pltpu.HBM((v_l, rows), bf), row, row, row),
             in_specs=[vmem_spec],
-            out_specs=(pl.BlockSpec((BLOCK, rows), lambda i: (i, 0)), vmem_spec),
+            out_specs=(any_spec,) * 4,
+            scratch_shapes=[pltpu.VMEM((SLOTS, BLOCK, rows), bf)] + [pltpu.VMEM((1, rows), f32)] * 3 + [
+                dma((SLOTS,)), dma((3,))],
             compiler_params=pltpu.CompilerParams(vmem_limit_bytes=8 * 2 ** 20),
         )(logits)
-        return stats[0], stats[1], stats[2], logprobs.T
+        return log_norm.reshape(rows), entropy.reshape(rows), target_lp.reshape(rows), logprobs.T
 
     return jax.shard_map(device_step, mesh=mesh, in_specs=(P('dp', None), P(None, ('tp', 'tp2')), P(None, ('tp', 'tp2')), P('tp', 'tp2'), P(None), P('tp2', 'tp'), P('dp'), P('dp')), out_specs=(P('dp'), P('dp'), P('dp'), P('dp', ('tp', 'tp2'))), check_vma=False)

time: 683 us -> 674 us (0.987)
  Pallas kernels: 678 us -> 671 us
    pallas_call x2, Pallas kernels: 678 us -> 671 us  [the longest x1 665 us: device_step(): pl.pallas_call(functools.partial(head_kernel, n_tp, v_l, ends), out_shape...]
where the time goes in v2:
time: 674 us; the launch traced here: 672 us
  Pallas kernels  671 us (100%)
    pallas_call x1, Pallas kernels, device_step(): pl.pallas_call(functools.partial(head_kernel, n_tp, v_l, ends), out_shape...  665 us

profile of v2, /device:TPU:0, one launch (start us, length us, event | category | flops | bytes accessed | tf_op | source)
XLA Modules:
  0.0 672.0 jit_solution(5690155372023177432)
XLA Ops:
  0.6 664.6 %shard_map.111 = (f32[19000,512]{1,0:T(8,128)S(1)}, bf16[18992,768]{1,0:T(8,128)(2,1)}) custom-call(bf16[4,128,1536]{2,1,0:T(8,128)(2,1)} %bitcast.14, bf16[1120,1536]{1,0:T(8,128)(2,1)} %bitcast.12, bf16[1120,1536]{1,0:T(8,128)(2,1)} %bitcast.13, bf16[2240,768]{1,0:T(8,128)(2,1)} %wd.1, f32[12,128]{1,0:T(8,128)} %bitcast.15, f32[1,512]{1,0:T(1,128)} %bitcast.16, ...), custom_call_target="tpu_custom_call" | custom-call | tf_op jit(solution)/shard_map/pallas_call | solution.py:336
  665.3 6.7 %shard_map.112 = (bf16[18992,512]{1,0:T(8,128)(2,1)}, f32[1,512]{1,0:T(1,128)}, f32[1,512]{1,0:T(1,128)}, f32[1,512]{1,0:T(1,128)}) custom-call(f32[19000,512]{1,0:T(8,128)S(1)} %get-tuple-element.9.logits), custom_call_target="tpu_custom_call" | custom-call | tf_op jit(solution)/shard_map/pallas_call | solution.py:377

commit v3 on v2

--- a/solution.py
+++ b/solution.py
@@ -12,7 +12,7 @@
 MESH = pl.DeviceIdType.MESH
 CHUNK = 512
 SUB = 64
-EARLY = 10
+EARLY = 12
 DEPTH = 3
 BLOCK = 512
 SLOTS = 6
@@ -54,6 +54,17 @@
     def dev(dt, dy):
         return {'tp': lax.rem(tp + dt, n_tp), 'tp2': lax.rem(y + dy, 2)}
 
+    def load(src, dst, k):
+        cp = pltpu.make_async_copy(src, dst, load_sem.at[k])
+        cp.start()
+        return cp
+
+    own_ff = pl.ds(pl.multiple_of(y * ff_l, 16), ff_l)
+    oth_ff = pl.ds(pl.multiple_of(oy * ff_l, 16), ff_l)
+    loads = [load(hidden, hid_v, 0), load(wg, wg_v, 1), load(wu, wu_v, 2),
+             load(wd.at[own_ff, :], wd_v.at[0], 3), load(wd.at[oth_ff, :], wd_v.at[1], 4),
+             load(temp, temp_v, 5), load(target, tgt_v, 6), load(gain, gain_v, 7)]
+
     barrier = pltpu.get_barrier_semaphore()
     for dt, dy in peers:
         pl.semaphore_signal(barrier, inc=1, device_id=dev(dt, dy), device_id_type=MESH)
@@ -73,19 +84,10 @@
         at = sum(ends[:i])
         return send(n_full * CHUNK + at, ends[i], e_oth.at[pl.ds(at, ends[i]), :], n_full + i)
 
-    ship(0).start()
-    ship(1).start()
-
-    def load(src, dst, k):
-        cp = pltpu.make_async_copy(src, dst, load_sem.at[k])
-        cp.start()
-        return cp
-
-    own_ff = pl.ds(pl.multiple_of(y * ff_l, 16), ff_l)
-    oth_ff = pl.ds(pl.multiple_of(oy * ff_l, 16), ff_l)
-    loads = [load(hidden, hid_v, 0), load(wg, wg_v, 1), load(wu, wu_v, 2),
-             load(wd.at[own_ff, :], wd_v.at[0], 3), load(wd.at[oth_ff, :], wd_v.at[1], 4),
-             load(temp, temp_v, 5), load(target, tgt_v, 6), load(gain, gain_v, 7)]
+    for c in range(4):
+        ship(c).start()
+
+    ship(0).wait()
     for cp in loads:
         cp.wait()
 
@@ -103,7 +105,7 @@
         src_ref=a_own, dst_ref=a_oth, send_sem=a_sem.at[0], recv_sem=a_sem.at[1],
         device_id=other, device_id_type=MESH)
     a_copy.start()
-    for c in range(2, 6):
+    for c in range(4, 8):
         ship(c).start()
 
     run_m[...] = jnp.full(run_m.shape, NEG, jnp.float32)
@@ -136,7 +138,7 @@
         src_ref=y_sum, dst_ref=y_oth, send_sem=s_sem.at[0], recv_sem=s_sem.at[1],
         device_id=other, device_id_type=MESH)
     s_copy.start()
-    for c in range(6, EARLY):
+    for c in range(8, EARLY):
         ship(c).start()
     s_copy.wait()
 
@@ -194,16 +196,26 @@
         run_d[...] = run_d[...] * keep + jnp.sum(p * tiles, axis=0)
         run_t[...] += jnp.sum(hit, axis=0)
 
+    def came(c, slot):
+        return pltpu.make_async_copy(
+            recv.at[pl.ds(pl.multiple_of(c * CHUNK, 16), CHUNK), :], w_oth.at[slot], oth_sem.at[slot])
+
+    def compute(c, slot):
+        own(c, slot).wait()
+        came(c, slot).wait()
+        acc = nn(w_own[slot], x_t[y]) + nn(w_oth[slot], x_t[oy])
+        logits[pl.ds(pl.multiple_of(c * CHUNK, 16), CHUNK), :] = acc * inv_t
+
+        @pl.loop(0, CHUNK // SUB)
+        def _(k):
+            update(c * CHUNK + k * SUB, SUB)
+
     own_end.start()
-    own(0, 0).start()
 
     @pl.loop(0, n_full)
     def _(c):
         slot = lax.rem(c, 2)
-
-        @pl.when(c + 1 < n_full)
-        def _():
-            own(c + 1, lax.rem(c + 1, 2)).start()
+        own(c, slot).start()
 
         @pl.when((c + DEPTH >= EARLY) & (c + DEPTH < n_full))
         def _():
@@ -214,19 +226,17 @@
             def _():
                 ship_end(i).start()
 
-        own(c, slot).wait()
-        ship(c).wait()
-        came = pltpu.make_async_copy(
-            recv.at[pl.ds(pl.multiple_of(c * CHUNK, 16), CHUNK), :], w_oth.at[slot], oth_sem)
-        came.start()
-        came.wait()
-        acc = nn(w_own[slot], x_t[y]) + nn(w_oth[slot], x_t[oy])
-        logits[pl.ds(pl.multiple_of(c * CHUNK, 16), CHUNK), :] = acc * inv_t
-
-        @pl.loop(0, CHUNK // SUB)
-        def _(k):
-            update(c * CHUNK + k * SUB, SUB)
-
+        @pl.when(c > 0)
+        def _():
+            ship(c).wait()
+
+        came(c, slot).start()
+
+        @pl.when(c > 0)
+        def _():
+            compute(c - 1, lax.rem(c + 1, 2))
+
+    compute(n_full - 1, (n_full - 1) % 2)
     at = n_full * CHUNK
     own_end.wait()
     logits[at:at + n_end, :] = nn(e_own[...], x_t[y])
@@ -246,7 +256,6 @@
     st_all[me, 1:2, :] = jnp.sum(run_s[...] * keep, axis=0, keepdims=True)
     st_all[me, 2:3, :] = jnp.sum(run_d[...] * keep, axis=0, keepdims=True)
     st_all[me, 3:4, :] = jnp.sum(run_t[...], axis=0, keepdims=True)
-    st_all[me, 4:8, :] = jnp.zeros((4, rows), jnp.float32)
     st_copies = []
     for i, (dt, dy) in enumerate(peers):
         cp = pltpu.make_async_remote_copy(
@@ -363,11 +372,11 @@
                 pltpu.VMEM((8, rows), f32),
                 pltpu.VMEM((8, rows), f32),
                 pltpu.VMEM((8, rows), f32),
-                pltpu.VMEM((n_tp * 2, 8, rows), f32),
+                pltpu.VMEM((n_tp * 2, 4, rows), f32),
                 dma((8,)), dma((n_sends,)), dma((n_sends,)), dma((2,)),
                 dma((n_tp - 1,)), dma((n_tp - 1,)), dma((2,)),
                 dma((n_tp - 1,)), dma((n_tp - 1,)),
-                dma((2,)), dma(()), dma(()), dma((7,)), dma((7,)),
+                dma((2,)), dma((2,)), dma(()), dma((7,)), dma((7,)),
             ],
             compiler_params=pltpu.CompilerParams(
                 collective_id=0, has_side_effects=True, vmem_limit_bytes=25 * 2 ** 20),

time: 674 us -> 672 us (level)
  no operation moved by 1% of the time
where the time goes in v3:
time: 672 us
  Pallas kernels  671 us (100%)
    pallas_call x1, Pallas kernels, device_step(): pl.pallas_call(functools.partial(head_kernel, n_tp, v_l, ends), out_shape...  664 us

profile of v3, /device:TPU:0, one launch (start us, length us, event | category | flops | bytes accessed | tf_op | source)
XLA Modules:
  0.0 671.8 jit_solution(16577775133720930241)
XLA Ops:
  0.6 664.4 %shard_map.111 = (f32[19000,512]{1,0:T(8,128)S(1)}, bf16[18992,768]{1,0:T(8,128)(2,1)}) custom-call(bf16[4,128,1536]{2,1,0:T(8,128)(2,1)} %bitcast.14, bf16[1120,1536]{1,0:T(8,128)(2,1)} %bitcast.12, bf16[1120,1536]{1,0:T(8,128)(2,1)} %bitcast.13, bf16[2240,768]{1,0:T(8,128)(2,1)} %wd.1, f32[12,128]{1,0:T(8,128)} %bitcast.15, f32[1,512]{1,0:T(1,128)} %bitcast.16, ...), custom_call_target="tpu_custom_call" | custom-call | tf_op jit(solution)/shard_map/pallas_call | solution.py:345
  665.1 6.7 %shard_map.112 = (bf16[18992,512]{1,0:T(8,128)(2,1)}, f32[1,512]{1,0:T(1,128)}, f32[1,512]{1,0:T(1,128)}, f32[1,512]{1,0:T(1,128)}) custom-call(f32[19000,512]{1,0:T(8,128)S(1)} %get-tuple-element.9.logits), custom_call_target="tpu_custom_call" | custom-call | tf_op jit(solution)/shard_map/pallas_call | solution.py:386

commit v4 on v3

--- a/solution.py
+++ b/solution.py
@@ -66,9 +66,10 @@
              load(temp, temp_v, 5), load(target, tgt_v, 6), load(gain, gain_v, 7)]
 
     barrier = pltpu.get_barrier_semaphore()
-    for dt, dy in peers:
+    near = [(dt, dy) for dt, dy in peers if not dt or not dy]
+    for dt, dy in near:
         pl.semaphore_signal(barrier, inc=1, device_id=dev(dt, dy), device_id_type=MESH)
-    pl.semaphore_wait(barrier, len(peers))
+    pl.semaphore_wait(barrier, len(near))
 
     def send(row, width, dst, k):
         return pltpu.make_async_remote_copy(

time: 672 us -> 671 us (level)
  no operation moved by 1% of the time
where the time goes in v4:
time: 671 us
  Pallas kernels  671 us (100%)
    pallas_call x1, Pallas kernels, device_step(): pl.pallas_call(functools.partial(head_kernel, n_tp, v_l, ends), out_shape...  664 us

profile of v4, /device:TPU:0, one launch (start us, length us, event | category | flops | bytes accessed | tf_op | source)
XLA Modules:
  0.0 671.2 jit_solution(15915603862946841286)
XLA Ops:
  0.6 663.8 %shard_map.111 = (f32[19000,512]{1,0:T(8,128)S(1)}, bf16[18992,768]{1,0:T(8,128)(2,1)}) custom-call(bf16[4,128,1536]{2,1,0:T(8,128)(2,1)} %bitcast.14, bf16[1120,1536]{1,0:T(8,128)(2,1)} %bitcast.12, bf16[1120,1536]{1,0:T(8,128)(2,1)} %bitcast.13, bf16[2240,768]{1,0:T(8,128)(2,1)} %wd.1, f32[12,128]{1,0:T(8,128)} %bitcast.15, f32[1,512]{1,0:T(1,128)} %bitcast.16, ...), custom_call_target="tpu_custom_call" | custom-call | tf_op jit(solution)/shard_map/pallas_call | solution.py:346
  664.5 6.7 %shard_map.112 = (bf16[18992,512]{1,0:T(8,128)(2,1)}, f32[1,512]{1,0:T(1,128)}, f32[1,512]{1,0:T(1,128)}, f32[1,512]{1,0:T(1,128)}) custom-call(f32[19000,512]{1,0:T(8,128)S(1)} %get-tuple-element.9.logits), custom_call_target="tpu_custom_call" | custom-call | tf_op jit(solution)/shard_map/pallas_call | solution.py:387

commit v5 on v4

--- a/solution.py
+++ b/solution.py
@@ -258,7 +258,7 @@
     st_all[me, 2:3, :] = jnp.sum(run_d[...] * keep, axis=0, keepdims=True)
     st_all[me, 3:4, :] = jnp.sum(run_t[...], axis=0, keepdims=True)
     st_copies = []
-    for i, (dt, dy) in enumerate(peers):
+    for i, (dt, dy) in enumerate(sorted(peers, key=lambda p: -(p[0] > 0) - p[1])):
         cp = pltpu.make_async_remote_copy(
             src_ref=st_all.at[me], dst_ref=st_all.at[me],
             send_sem=st_send.at[i], recv_sem=st_got.at[i],

time: 671 us -> 671 us (level)
  no operation moved by 1% of the time
where the time goes in v5:
time: 671 us
  Pallas kernels  670 us (100%)
    pallas_call x1, Pallas kernels, device_step(): pl.pallas_call(functools.partial(head_kernel, n_tp, v_l, ends), out_shape...  664 us

profile of v5, /device:TPU:0, one launch (start us, length us, event | category | flops | bytes accessed | tf_op | source)
XLA Modules:
  0.0 671.1 jit_solution(18150138130954482380)
XLA Ops:
  0.6 663.8 %shard_map.111 = (f32[19000,512]{1,0:T(8,128)S(1)}, bf16[18992,768]{1,0:T(8,128)(2,1)}) custom-call(bf16[4,128,1536]{2,1,0:T(8,128)(2,1)} %bitcast.14, bf16[1120,1536]{1,0:T(8,128)(2,1)} %bitcast.12, bf16[1120,1536]{1,0:T(8,128)(2,1)} %bitcast.13, bf16[2240,768]{1,0:T(8,128)(2,1)} %wd.1, f32[12,128]{1,0:T(8,128)} %bitcast.15, f32[1,512]{1,0:T(1,128)} %bitcast.16, ...), custom_call_target="tpu_custom_call" | custom-call | tf_op jit(solution)/shard_map/pallas_call | solution.py:346
  664.4 6.7 %shard_map.112 = (bf16[18992,512]{1,0:T(8,128)(2,1)}, f32[1,512]{1,0:T(1,128)}, f32[1,512]{1,0:T(1,128)}, f32[1,512]{1,0:T(1,128)}) custom-call(f32[19000,512]{1,0:T(8,128)S(1)} %get-tuple-element.9.logits), custom_call_target="tpu_custom_call" | custom-call | tf_op jit(solution)/shard_map/pallas_call | solution.py:387
